TPU v7x, 32 devices: a whole 2x2x4 slice. The times are simulated.
32 devices in a mesh: section: 4 (over y, x), row: 8 (over z, core).
Axes of the slice: x: 2, y: 2, z: 4, core: 2. Of those that a mesh axis runs over, the one named last changes fastest.
Arguments:
- omega: bfloat16 [2048, 8192], P('section', 'row'), may hold values from -0.5 to 0.5
- basis: bfloat16 [8192, 1024], P('row', 'section'), may hold values from -6 to 6
- vectors: bfloat16 [4, 8192], P(None, 'row'), may hold values from -6 to 6
Outputs:
- ortho: float32 [4, 8192], P(None, ('row', 'section'))
- coeffs: float32 [4, 1024], P(None, 'section')
All inputs are finite; a program needn't handle non-finite values.
Results may differ from a plain program's by a relative error of at most 0.0021.
Values may be sent and summed in bfloat16 or wider, within the bound.
A program may use at most 64 MiB of HBM per device.

v0:
```python
import jax
import jax.numpy as jnp
from jax import lax
from jax.sharding import PartitionSpec as P


def from_behind(value, axis, steps):
    count = lax.axis_size(axis)
    initial, last = (max(0, -steps), min(count, count - steps))
    return lax.ppermute(value, axis, [(source, source + steps) for source in range(initial, last)])


def from_root(value, axis, source):
    kept = jnp.where(lax.axis_index(axis) == source, value, 0).astype(value.dtype)
    return lax.psum(kept, axis)


def lower_solve(factor, right):
    return lax.linalg.triangular_solve(factor, right, left_side=True, lower=True, transpose_a=False)


def factor_solve(factor, right):
    half = lower_solve(factor, right)
    return lax.linalg.triangular_solve(factor, half, left_side=True, lower=True, transpose_a=True)


def body(omega, basis, vectors):
    hi = lax.Precision.HIGHEST
    sections = lax.axis_size("section")
    my_section = lax.axis_index("section")
    whole = lax.all_gather(omega, "section", axis=0, tiled=True)
    sketch = lax.psum_scatter(
        jnp.dot(whole, basis, preferred_element_type=jnp.float32),
        "row",
        scatter_dimension=0,
        tiled=True,
    )
    probe_term = lax.dot_general(
        vectors, whole, (((1,), (1,)), ((), ())), preferred_element_type=jnp.float32
    )
    probe = lax.psum_scatter(probe_term, "row", scatter_dimension=1, tiled=True)
    gram = lax.psum(jnp.dot(sketch.T, sketch, precision=hi), "row")
    factor = jnp.linalg.cholesky(gram)

    def project(current):
        inner = jnp.dot(current, sketch, precision=hi)
        inner = lax.psum(inner, "row")
        coef = factor_solve(factor, inner.T).T
        return (coef, current - jnp.dot(coef, sketch.T, precision=hi))

    def advance(step, carry):
        current, kept = carry
        coef, moved = project(current)
        active = my_section == step
        kept = jnp.where(active, coef, kept)
        moved = jnp.where(active, moved, current)
        return (from_behind(moved, "section", 1), kept)

    start_coef = jnp.zeros((vectors.shape[0], basis.shape[1]), jnp.float32)
    probe, kept = lax.fori_loop(0, sections - 1, advance, (probe, start_coef))
    coef, moved = project(probe)
    finished = my_section == sections - 1
    kept = jnp.where(finished, coef, kept)
    final = from_root(moved, "section", sections - 1)
    rounded = kept.astype(jnp.bfloat16)
    own_term = lax.dot_general(
        rounded, basis, (((1,), (1,)), ((), ())), preferred_element_type=jnp.float32
    )
    removed = lax.psum_scatter(own_term, "section", scatter_dimension=1, tiled=True)
    width = removed.shape[1]
    mine = lax.dynamic_slice_in_dim(vectors, my_section * width, width, 1)
    remain = mine.astype(jnp.float32) - removed
    small = lax.psum(jnp.dot(final, final.T, precision=hi), "row")
    lower = jnp.linalg.cholesky(small)
    ortho = lower_solve(lower, remain)
    return (ortho, kept)


def solution(mesh):
    return jax.shard_map(
        body,
        mesh=mesh,
        in_specs=(P("section", "row"), P("row", "section"), P(None, "row")),
        out_specs=(P(None, ("row", "section")), P(None, "section")),
        check_vma=False,
    )
```

profile of v0, /device:TPU:0, one launch (start us, length us, event | category | flops | bytes accessed | tf_op | source)
XLA Modules:
  0.0 442.4 jit_solution(2750653464107480190)
XLA Ops:
  8.0 57.2 %all-gather.2.cloned.1.call-done = bf16[2048,1024]{1,0:T(8,128)(2,1)} async-done(((bf16[512,1024]{1,0:T(8,128)(2,1)}), bf16[2048,1024]{1,0:T(8,128)(2,1)}) %all-gather.2.cloned.1.call-update) | async-done | bytes 4194320 | tf_op jit(solution)/shard_map/all_gather | solution.py:31
  65.2 4.8 %fusion.36 = f32[2048,256]{1,0:T(8,128)} fusion(bf16[2048,1024]{1,0:T(8,128)(2,1)} %all-gather.2.cloned.1.call-done, bf16[1024,256]{1,0:T(8,128)(2,1)S(1)} %copy-done), kind=kOutput, calls=%fused_computation.78 | convolution fusion | flops 1073741824 | bytes 6815744 | tf_op jit(solution)/shard_map/dot_general | solution.py:33
  70.0 4.4 convolution_bitcast_fusion
  74.5 31.6 %reduce-scatter.8.cloned.1.call-done = f32[256,256]{1,0:T(8,128)} async-done(((f32[2048,256]{1,0:T(8,128)}), f32[256,256]{1,0:T(8,128)}) %reduce-scatter.8.cloned.1.call-update) | async-done | bytes 262160 | tf_op jit(solution)/shard_map/reduce_scatter | solution.py:32
  106.1 2.4 fusion.37
  108.8 30.9 %reduce-scatter.10.cloned.1.call-done = f32[256,4]{1,0:T(8,128)} async-done(((f32[2048,4]{1,0:T(8,128)}), f32[256,4]{1,0:T(8,128)}) %reduce-scatter.10.cloned.1.call-update) | async-done | bytes 4112
  140.7 54.8 %all-reduce.3.cloned.1.call-done = f32[256,256]{0,1:T(8,128)} async-done(((f32[256,256]{0,1:T(8,128)}), f32[256,256]{0,1:T(8,128)}) %all-reduce.3.cloned.1.call-update) | async-done | bytes 262160 | tf_op jit(solution)/shard_map/psum | solution.py:42
  197.6 11.7 %cholesky.64 = f32[128,128]{1,0:T(8,128)S(1)} custom-call(f32[128,128]{1,0:T(8,128)S(1)} %cholesky.153), custom_call_target="Cholesky" | custom-call | tf_op jit(solution)/shard_map/jit(cholesky)/cholesky | solution.py:43
  209.4 9.8 %custom-call.23 = f32[1,128,128]{1,2,0:T(8,128)S(1)} custom-call(f32[1,128,128]{2,1,0:T(8,128)S(1)} %get-tuple-element.206), custom_call_target="InvertDiagBlocksLowerTriangular" | custom-call | tf_op jit(solution)/shard_map/jit(cholesky)/cholesky | solution.py:43
  219.7 11.7 %cholesky.131 = f32[128,128]{1,0:T(8,128)S(1)} custom-call(f32[128,128]{1,0:T(8,128)S(1)} %convolution_subtract_fusion.3), custom_call_target="Cholesky" | custom-call | tf_op jit(solution)/shard_map/jit(cholesky)/cholesky | solution.py:43
  233.5 4.2 while.27
  234.4 1.3 bitcast_dynamic-update-slice_fusion.4
  236.4 1.3 bitcast_dynamic-update-slice_fusion.4
  237.8 19.7 %custom-call.31 = f32[2,128,128]{1,2,0:T(8,128)S(1)} custom-call(f32[2,128,128]{2,1,0:T(8,128)S(1)} %get-tuple-element.168), custom_call_target="InvertDiagBlocksLowerTriangular" | custom-call | tf_op jit(solution)/shard_map/triangular_solve/custom-call.4 | solution.py:24
  257.4 133.4 %while.26 = (s32[]{:T(128)}, f32[4,256]{1,0:T(4,128)S(1)}, f32[4,256]{1,0:T(4,128)S(1)}, s32[]{:T(128)}, f32[256,256]{1,0:T(8,128)S(1)}, /*index=5*/f32[256,256]{1,0:T(8,128)S(1)}, s32[]{:T(128)}, s32[]{:T(128)}, s32[]{:T(128)}) while((s32[]{:T(128)}, f32[4,256]{1,0:T(4,128)S(1)}, f32[4,256]{1,0:T(4,128)S(1)}, s32[]{:T(128)}, ...), condition=%wide.region_9.12_spmd.clone, body=%wide.region_7.0_spmd.clone.sunk | while | flops 11149320 | bytes 1659231 | solution.py:60
  257.6 4.1 while.28
  261.6 19.7 %custom-call.37 = f32[2,128,128]{1,2,0:T(8,128)S(1)} custom-call(f32[2,128,128]{2,1,0:T(8,128)S(1)} %get-tuple-element.303), custom_call_target="InvertDiagBlocksLowerTriangular" | custom-call | tf_op jit(solution)/shard_map/while/body/eval_jaxpr/triangular_solve/custom-call.4 | solution.py:24
  281.5 13.7 %psum.45 = f32[256,4]{0,1:T(4,128)S(1)} all-reduce(f32[256,4]{0,1:T(4,128)S(1)} %fusion.99), channel_id=1, replica_groups=mesh['section'=4,'row'=8] {'row'}, use_global_device_ids=true, to_apply=%region_8.8 | all-reduce | flops 1024 | bytes 8192 | tf_op jit(solution)/shard_map/while/body/eval_jaxpr/psum | solution.py:47
  296.7 3.4 collective-permute-start
  301.5 4.1 while.28
  302.2 1.3 bitcast_dynamic-update-slice_fusion.5
  304.2 1.3 bitcast_dynamic-update-slice_fusion.5
  305.6 19.7 %custom-call.37 = f32[2,128,128]{1,2,0:T(8,128)S(1)} custom-call(f32[2,128,128]{2,1,0:T(8,128)S(1)} %get-tuple-element.303), custom_call_target="InvertDiagBlocksLowerTriangular" | custom-call | tf_op jit(solution)/shard_map/while/body/eval_jaxpr/triangular_solve/custom-call.4 | solution.py:24
  325.5 13.6 %psum.45 = f32[256,4]{0,1:T(4,128)S(1)} all-reduce(f32[256,4]{0,1:T(4,128)S(1)} %fusion.99), channel_id=1, replica_groups=mesh['section'=4,'row'=8] {'row'}, use_global_device_ids=true, to_apply=%region_8.8 | all-reduce | flops 1024 | bytes 8192 | tf_op jit(solution)/shard_map/while/body/eval_jaxpr/psum | solution.py:47
  340.6 4.2 collective-permute-start
  346.2 4.1 while.28
  350.3 19.7 %custom-call.37 = f32[2,128,128]{1,2,0:T(8,128)S(1)} custom-call(f32[2,128,128]{2,1,0:T(8,128)S(1)} %get-tuple-element.303), custom_call_target="InvertDiagBlocksLowerTriangular" | custom-call | tf_op jit(solution)/shard_map/while/body/eval_jaxpr/triangular_solve/custom-call.4 | solution.py:24
  370.2 13.6 %psum.45 = f32[256,4]{0,1:T(4,128)S(1)} all-reduce(f32[256,4]{0,1:T(4,128)S(1)} %fusion.99), channel_id=1, replica_groups=mesh['section'=4,'row'=8] {'row'}, use_global_device_ids=true, to_apply=%region_8.8 | all-reduce | flops 1024 | bytes 8192 | tf_op jit(solution)/shard_map/while/body/eval_jaxpr/psum | solution.py:47
  385.2 4.3 collective-permute-start
  391.1 13.6 %psum.40 = f32[256,4]{0,1:T(4,128)S(1)} all-reduce(f32[256,4]{0,1:T(4,128)S(1)} %fusion.38), channel_id=1, replica_groups=mesh['section'=4,'row'=8] {'row'}, use_global_device_ids=true, to_apply=%region_10.13 | all-reduce | flops 1024 | bytes 8192 | tf_op jit(solution)/shard_map/psum | solution.py:47
  407.2 11.0 %psum.41 = f32[4,256]{1,0:T(4,128)S(1)} all-reduce(f32[4,256]{1,0:T(4,128)S(1)} %fusion.10), channel_id=1, replica_groups=mesh['section'=4,'row'=8] {'section'}, use_global_device_ids=true, to_apply=%region_11.14 | all-reduce | flops 1024 | bytes 8192 | tf_op jit(solution)/shard_map/psum | solution.py:15
  418.3 13.6 %psum.42 = f32[4,4]{0,1:T(4,128)S(1)} all-reduce(f32[4,4]{0,1:T(4,128)S(1)} %fusion.39), channel_id=1, replica_groups=mesh['section'=4,'row'=8] {'row'}, use_global_device_ids=true, to_apply=%region_12.15 | all-reduce | flops 16 | bytes 128 | tf_op jit(solution)/shard_map/psum | solution.py:73
  (116 shorter events, 32.2 us)
Async XLA Ops:
  7.2 58.0 %copy-start = (bf16[1024,256]{1,0:T(8,128)(2,1)S(1)}, bf16[1024,256]{1,0:T(8,128)(2,1)}, u32[]{:S(2)}) copy-start(bf16[1024,256]{1,0:T(8,128)(2,1)} %param.10) | copy-start | bytes 1572868
  7.2 58.0 %all-gather.2.cloned.1.call-start = ((), (), s32[]{:S(2)}) async-start(), calls=%async_computation.3 | async-start | bytes 5242880 | tf_op jit(solution)/shard_map/all_gather | solution.py:31
  7.9 62.1 %copy-start.3 = (bf16[4,1024]{1,0:T(4,128)(2,1)S(1)}, bf16[4,1024]{1,0:T(4,128)(2,1)}, u32[]{:S(2)}) copy-start(bf16[4,1024]{1,0:T(4,128)(2,1)} %param.11) | copy-start | bytes 24580
  7.9 98.2 %reduce-scatter.8.cloned.1.call-start = ((), (), s32[]{:S(2)}) async-start(), calls=%async_computation.4 | async-start | bytes 2359296 | tf_op jit(solution)/shard_map/reduce_scatter | solution.py:32
  70.0 69.7 %reduce-scatter.10.cloned.1.call-start = ((), (), s32[]{:S(2)}) async-start(), calls=%async_computation.6 | async-start | bytes 1179648
  74.5 121.0 %all-reduce.3.cloned.1.call-start = ((), (), s32[]{:S(2)}) async-start(), calls=%async_computation.5 | async-start | bytes 524288 | tf_op jit(solution)/shard_map/psum | solution.py:42
  106.1 151.3 %copy-start.1 = (f32[256,256]{1,0:T(8,128)S(1)}, f32[256,256]{1,0:T(8,128)}, u32[]{:S(2)}) copy-start(f32[256,256]{1,0:T(8,128)} %reduce-scatter.8.cloned.1.call-done) | copy-start | bytes 786436
  108.5 325.5 %reduce-scatter.12.cloned.1.call-start = ((), (), s32[]{:S(2)}) async-start(), calls=%async_computation.7 | async-start | bytes 655360
  296.7 4.7 %collective-permute-start = (f32[4,256]{1,0:T(4,128)S(1)}, f32[4,256]{1,0:T(4,128)S(1)}, u32[]{:S(2)}, u32[]{:S(2)}) collective-permute-start(f32[4,256]{1,0:T(4,128)S(1)} %fusion.104), channel_id=1, source_target_pairs={{0,8},{8,16},{16,24},{1,9},{9,17},{17,25},{2,10},{10,18},{18,26},{... | collective-permute-start | bytes 12296 | tf_op jit(solution)/shard_map/while/body/eval_jaxpr/ppermute | solution.py:10
  340.6 5.6 %collective-permute-start = (f32[4,256]{1,0:T(4,128)S(1)}, f32[4,256]{1,0:T(4,128)S(1)}, u32[]{:S(2)}, u32[]{:S(2)}) collective-permute-start(f32[4,256]{1,0:T(4,128)S(1)} %fusion.104), channel_id=1, source_target_pairs={{0,8},{8,16},{16,24},{1,9},{9,17},{17,25},{2,10},{10,18},{18,26},{... | collective-permute-start | bytes 12296 | tf_op jit(solution)/shard_map/while/body/eval_jaxpr/ppermute | solution.py:10
  385.2 5.6 %collective-permute-start = (f32[4,256]{1,0:T(4,128)S(1)}, f32[4,256]{1,0:T(4,128)S(1)}, u32[]{:S(2)}, u32[]{:S(2)}) collective-permute-start(f32[4,256]{1,0:T(4,128)S(1)} %fusion.104), channel_id=1, source_target_pairs={{0,8},{8,16},{16,24},{1,9},{9,17},{17,25},{2,10},{10,18},{18,26},{... | collective-permute-start | bytes 12296 | tf_op jit(solution)/shard_map/while/body/eval_jaxpr/ppermute | solution.py:10
  405.9 30.0 %copy-start.2 = (f32[4,256]{1,0:T(4,128)}, f32[4,256]{1,0:T(4,128)S(1)}, u32[]{:S(2)}) copy-start(f32[4,256]{1,0:T(4,128)S(1)} %bitcast_select_fusion.1) | copy-start | bytes 12292
Sparse Core Ops, SparseCore 0:
  9.8 55.2 all-gather.1
  70.1 35.9 reduce-scatter.7
  108.4 31.2 reduce-scatter.9
  141.9 53.5 all-reduce.2
  407.1 25.7 reduce-scatter.11
where the time goes:
time: 443 us; the launch traced here: 442 us
  waiting for transfers between devices  179 us (40%)
  other arithmetic  116 us (26%)
  blocking collectives  79.1 us (18%)
  matrix products  20.6 us (5%)
  local copies, waits for them, and re-layouts  19.6 us (4%)
  between operations  15.2 us (3%)
  starting transfers between devices  12.4 us (3%)
    another operation x16, other arithmetic, factor_solve(): lax.linalg.triangular_solve(factor, half, left_side=True, lower=True, tra...  78.8 us
    all_gather x1, waiting for transfers between devices, body(): whole = lax.all_gather(omega, 'section', axis=0, tiled=True)  57.2 us
    psum x1, waiting for transfers between devices, body(): gram = lax.psum(jnp.dot(sketch.T, sketch, precision=hi), 'row')  54.8 us
    psum x4, blocking collectives, project(): inner = lax.psum(inner, 'row')  54.5 us
    another operation x6, other arithmetic, body(): factor = jnp.linalg.cholesky(gram)  34 us
    unnamed x7, waiting for transfers between devices  31.7 us
    reduce_scatter x1, waiting for transfers between devices, body(): lax.psum_scatter(jnp.dot(whole, basis, preferred_element_type=jnp.float32...  31.6 us
    another operation x28, local copies, waits for them, and re-layouts, factor_solve(): lax.linalg.triangular_solve(factor, half, left_side=True, lower=True, tra...  16.4 us
  transfers between devices with their start and end apart: 8, of which 7 were waited for; matrix products, arithmetic and copies ran while one was open for 2% of the time, Pallas kernels for 0%

commit v1 on v0

--- a/solution.py
+++ b/solution.py
@@ -39,7 +39,7 @@
         vectors, whole, (((1,), (1,)), ((), ())), preferred_element_type=jnp.float32
     )
     probe = lax.psum_scatter(probe_term, "row", scatter_dimension=1, tiled=True)
-    gram = lax.psum(jnp.dot(sketch.T, sketch, precision=hi), "row")
+    gram = jnp.sum(lax.all_gather(jnp.dot(sketch.T, sketch, precision=hi), "row"), axis=0)
     factor = jnp.linalg.cholesky(gram)
 
     def project(current):

time: 443 us -> 417 us (0.941)
  waiting for transfers between devices: 179 us -> 152 us
    psum x1 -> x0, waiting for transfers between devices: 54.8 us -> none  [body(): gram = lax.psum(jnp.dot(sketch.T, sketch, precision=hi), 'row')]
    all_gather x0 -> x1, waiting for transfers between devices: none -> 27.8 us  [body(): lax.all_gather(jnp.dot(sketch.T, sketch, precision=hi), 'row')]
where the time goes in v1:
time: 417 us
  waiting for transfers between devices  152 us (36%)
  other arithmetic  117 us (28%)
  blocking collectives  80.7 us (19%)
  matrix products  20.7 us (5%)
  local copies, waits for them, and re-layouts  18.6 us (4%)
  between operations  15.2 us (4%)
  starting transfers between devices  12.4 us (3%)
    another operation x16, other arithmetic, factor_solve(): lax.linalg.triangular_solve(factor, half, left_side=True, lower=True, tra...  78.8 us
    all_gather x1, waiting for transfers between devices, body(): whole = lax.all_gather(omega, 'section', axis=0, tiled=True)  57.2 us
    psum x4, blocking collectives, project(): inner = lax.psum(inner, 'row')  56.1 us
    another operation x6, other arithmetic, body(): factor = jnp.linalg.cholesky(gram)  34 us
    unnamed x7, waiting for transfers between devices  31.6 us
    reduce_scatter x1, waiting for transfers between devices, body(): lax.psum_scatter(jnp.dot(whole, basis, preferred_element_type=jnp.float32...  31.6 us
    all_gather x1, waiting for transfers between devices, body(): lax.all_gather(jnp.dot(sketch.T, sketch, precision=hi), 'row')  27.8 us
    another operation x28, local copies, waits for them, and re-layouts, factor_solve(): lax.linalg.triangular_solve(factor, half, left_side=True, lower=True, tra...  16.4 us
  transfers between devices with their start and end apart: 8, of which 7 were waited for; matrix products, arithmetic and copies ran while one was open for 2% of the time, Pallas kernels for 0%

profile of v1, /device:TPU:0, one launch (start us, length us, event | category | flops | bytes accessed | tf_op | source)
XLA Modules:
  0.0 416.8 jit_solution(15039774899359144012)
XLA Ops:
  8.0 57.2 %all-gather.4.cloned.1.call-done = bf16[2048,1024]{1,0:T(8,128)(2,1)} async-done(((bf16[512,1024]{1,0:T(8,128)(2,1)}), bf16[2048,1024]{1,0:T(8,128)(2,1)}) %all-gather.4.cloned.1.call-update) | async-done | bytes 4194320 | tf_op jit(solution)/shard_map/all_gather | solution.py:31
  65.2 4.8 %fusion.36 = f32[2048,256]{1,0:T(8,128)} fusion(bf16[2048,1024]{1,0:T(8,128)(2,1)} %all-gather.4.cloned.1.call-done, bf16[1024,256]{1,0:T(8,128)(2,1)S(1)} %copy-done), kind=kOutput, calls=%fused_computation.78 | convolution fusion | flops 1073741824 | bytes 6815744 | tf_op jit(solution)/shard_map/dot_general | solution.py:33
  70.0 4.4 %convolution_bitcast_fusion = f32[2048,4]{1,0:T(8,128)} fusion(bf16[4,1024]{1,0:T(4,128)(2,1)S(1)} %copy-done.3, bf16[2048,1024]{1,0:T(8,128)(2,1)} %all-gather.4.cloned.1.call-done), kind=kOutput, calls=%fused_computation.23 | convolution fusion | flops 16777216 | bytes 4235264
  74.5 31.6 %reduce-scatter.8.cloned.1.call-done = f32[256,256]{1,0:T(8,128)} async-done(((f32[2048,256]{1,0:T(8,128)}), f32[256,256]{1,0:T(8,128)}) %reduce-scatter.8.cloned.1.call-update) | async-done | bytes 262160 | tf_op jit(solution)/shard_map/reduce_scatter | solution.py:32
  106.1 2.4 fusion.37
  108.8 30.9 %reduce-scatter.10.cloned.1.call-done = f32[256,4]{1,0:T(8,128)} async-done(((f32[2048,4]{1,0:T(8,128)}), f32[256,4]{1,0:T(8,128)}) %reduce-scatter.10.cloned.1.call-update) | async-done | bytes 4112
  140.7 27.8 %all-gather.6.cloned.1.call-done = f32[2048,256]{1,0:T(8,128)} async-done(((f32[256,256]{1,0:T(8,128)}), f32[2048,256]{1,0:T(8,128)}) %all-gather.6.cloned.1.call-update) | async-done | bytes 2097168 | tf_op jit(solution)/shard_map/all_gather | solution.py:42
  168.5 1.8 reduce_sum.9
  170.5 11.7 %cholesky.64 = f32[128,128]{1,0:T(8,128)S(1)} custom-call(f32[128,128]{1,0:T(8,128)S(1)} %cholesky.153), custom_call_target="Cholesky" | custom-call | tf_op jit(solution)/shard_map/jit(cholesky)/cholesky | solution.py:43
  182.3 9.8 %custom-call.23 = f32[1,128,128]{1,2,0:T(8,128)S(1)} custom-call(f32[1,128,128]{2,1,0:T(8,128)S(1)} %get-tuple-element.206), custom_call_target="InvertDiagBlocksLowerTriangular" | custom-call | tf_op jit(solution)/shard_map/jit(cholesky)/cholesky | solution.py:43
  192.5 11.7 %cholesky.131 = f32[128,128]{1,0:T(8,128)S(1)} custom-call(f32[128,128]{1,0:T(8,128)S(1)} %convolution_subtract_fusion.3), custom_call_target="Cholesky" | custom-call | tf_op jit(solution)/shard_map/jit(cholesky)/cholesky | solution.py:43
  206.4 4.2 %while.27 = (s32[]{:T(128)}, f32[256,256]{1,0:T(8,128)S(1)}, s32[2,2]{1,0:T(2,128)S(1)}, f32[2,128,128]{2,1,0:T(8,128)S(1)}, s32[]{:T(128)}) while((s32[]{:T(128)}, f32[256,256]{1,0:T(8,128)S(1)}, s32[2,2]{1,0:T(2,128)S(1)}, f32[2,128,128]{2,1,0:T(8,128)S(1)}, s32[]{:T(128)}) %tuple.89), condition=%wide.while_cond.1.clone, body=%wide.while_body.1.clone.sunk | while | flops 2 | bytes 131189 | solution.py:24
  207.2 1.3 bitcast_dynamic-update-slice_fusion.4
  209.3 1.3 bitcast_dynamic-update-slice_fusion.4
  210.6 19.7 %custom-call.31 = f32[2,128,128]{1,2,0:T(8,128)S(1)} custom-call(f32[2,128,128]{2,1,0:T(8,128)S(1)} %get-tuple-element.168), custom_call_target="InvertDiagBlocksLowerTriangular" | custom-call | tf_op jit(solution)/shard_map/triangular_solve/custom-call.4 | solution.py:24
  230.3 135.0 %while.26 = (s32[]{:T(128)}, f32[4,256]{1,0:T(4,128)S(1)}, f32[4,256]{1,0:T(4,128)S(1)}, s32[]{:T(128)}, f32[256,256]{1,0:T(8,128)S(1)}, /*index=5*/f32[256,256]{1,0:T(8,128)S(1)}, s32[]{:T(128)}, s32[]{:T(128)}, s32[]{:T(128)}) while((s32[]{:T(128)}, f32[4,256]{1,0:T(4,128)S(1)}, f32[4,256]{1,0:T(4,128)S(1)}, s32[]{:T(128)}, ...), condition=%wide.region_9.12_spmd.clone, body=%wide.region_7.0_spmd.clone.sunk | while | flops 11149320 | bytes 1659231 | solution.py:60
  230.5 4.1 while.28
  233.2 1.3 bitcast_dynamic-update-slice_fusion.5
  234.5 19.7 %custom-call.37 = f32[2,128,128]{1,2,0:T(8,128)S(1)} custom-call(f32[2,128,128]{2,1,0:T(8,128)S(1)} %get-tuple-element.303), custom_call_target="InvertDiagBlocksLowerTriangular" | custom-call | tf_op jit(solution)/shard_map/while/body/eval_jaxpr/triangular_solve/custom-call.4 | solution.py:24
  254.4 15.3 %psum.37 = f32[256,4]{0,1:T(4,128)S(1)} all-reduce(f32[256,4]{0,1:T(4,128)S(1)} %fusion.99), channel_id=1, replica_groups=mesh['section'=4,'row'=8] {'row'}, use_global_device_ids=true, to_apply=%region_8.8 | all-reduce | flops 1024 | bytes 8192 | tf_op jit(solution)/shard_map/while/body/eval_jaxpr/psum | solution.py:47
  271.2 3.4 collective-permute-start
  276.0 4.1 while.28
  280.1 19.7 %custom-call.37 = f32[2,128,128]{1,2,0:T(8,128)S(1)} custom-call(f32[2,128,128]{2,1,0:T(8,128)S(1)} %get-tuple-element.303), custom_call_target="InvertDiagBlocksLowerTriangular" | custom-call | tf_op jit(solution)/shard_map/while/body/eval_jaxpr/triangular_solve/custom-call.4 | solution.py:24
  300.0 13.6 %psum.37 = f32[256,4]{0,1:T(4,128)S(1)} all-reduce(f32[256,4]{0,1:T(4,128)S(1)} %fusion.99), channel_id=1, replica_groups=mesh['section'=4,'row'=8] {'row'}, use_global_device_ids=true, to_apply=%region_8.8 | all-reduce | flops 1024 | bytes 8192 | tf_op jit(solution)/shard_map/while/body/eval_jaxpr/psum | solution.py:47
  315.0 4.2 %collective-permute-start = (f32[4,256]{1,0:T(4,128)S(1)}, f32[4,256]{1,0:T(4,128)S(1)}, u32[]{:S(2)}, u32[]{:S(2)}) collective-permute-start(f32[4,256]{1,0:T(4,128)S(1)} %fusion.104), channel_id=1, source_target_pairs={{0,8},{8,16},{16,24},{1,9},{9,17},{17,25},{2,10},{10,18},{18,26},{... | collective-permute-start | bytes 12296 | tf_op jit(solution)/shard_map/while/body/eval_jaxpr/ppermute | solution.py:10
  320.7 4.1 while.28
  324.7 19.7 %custom-call.37 = f32[2,128,128]{1,2,0:T(8,128)S(1)} custom-call(f32[2,128,128]{2,1,0:T(8,128)S(1)} %get-tuple-element.303), custom_call_target="InvertDiagBlocksLowerTriangular" | custom-call | tf_op jit(solution)/shard_map/while/body/eval_jaxpr/triangular_solve/custom-call.4 | solution.py:24
  344.6 13.6 %psum.37 = f32[256,4]{0,1:T(4,128)S(1)} all-reduce(f32[256,4]{0,1:T(4,128)S(1)} %fusion.99), channel_id=1, replica_groups=mesh['section'=4,'row'=8] {'row'}, use_global_device_ids=true, to_apply=%region_8.8 | all-reduce | flops 1024 | bytes 8192 | tf_op jit(solution)/shard_map/while/body/eval_jaxpr/psum | solution.py:47
  359.7 4.3 %collective-permute-start = (f32[4,256]{1,0:T(4,128)S(1)}, f32[4,256]{1,0:T(4,128)S(1)}, u32[]{:S(2)}, u32[]{:S(2)}) collective-permute-start(f32[4,256]{1,0:T(4,128)S(1)} %fusion.104), channel_id=1, source_target_pairs={{0,8},{8,16},{16,24},{1,9},{9,17},{17,25},{2,10},{10,18},{18,26},{... | collective-permute-start | bytes 12296 | tf_op jit(solution)/shard_map/while/body/eval_jaxpr/ppermute | solution.py:10
  365.5 13.6 %psum.32 = f32[256,4]{0,1:T(4,128)S(1)} all-reduce(f32[256,4]{0,1:T(4,128)S(1)} %fusion.38), channel_id=1, replica_groups=mesh['section'=4,'row'=8] {'row'}, use_global_device_ids=true, to_apply=%region_10.13 | all-reduce | flops 1024 | bytes 8192 | tf_op jit(solution)/shard_map/psum | solution.py:47
  381.7 10.9 %psum.33 = f32[4,256]{1,0:T(4,128)S(1)} all-reduce(f32[4,256]{1,0:T(4,128)S(1)} %fusion.10), channel_id=1, replica_groups=mesh['section'=4,'row'=8] {'section'}, use_global_device_ids=true, to_apply=%region_11.14 | all-reduce | flops 1024 | bytes 8192 | tf_op jit(solution)/shard_map/psum | solution.py:15
  392.8 13.6 %psum.34 = f32[4,4]{0,1:T(4,128)S(1)} all-reduce(f32[4,4]{0,1:T(4,128)S(1)} %fusion.39), channel_id=1, replica_groups=mesh['section'=4,'row'=8] {'row'}, use_global_device_ids=true, to_apply=%region_12.15 | all-reduce | flops 16 | bytes 128 | tf_op jit(solution)/shard_map/psum | solution.py:73
  (117 shorter events, 31.7 us)
Async XLA Ops:
  7.2 58.0 %copy-start = (bf16[1024,256]{1,0:T(8,128)(2,1)S(1)}, bf16[1024,256]{1,0:T(8,128)(2,1)}, u32[]{:S(2)}) copy-start(bf16[1024,256]{1,0:T(8,128)(2,1)} %param.10) | copy-start | bytes 1572868
  7.2 58.0 %all-gather.4.cloned.1.call-start = ((), (), s32[]{:S(2)}) async-start(), calls=%async_computation.3 | async-start | bytes 5242880 | tf_op jit(solution)/shard_map/all_gather | solution.py:31
  7.9 62.1 %copy-start.3 = (bf16[4,1024]{1,0:T(4,128)(2,1)S(1)}, bf16[4,1024]{1,0:T(4,128)(2,1)}, u32[]{:S(2)}) copy-start(bf16[4,1024]{1,0:T(4,128)(2,1)} %param.11) | copy-start | bytes 24580
  7.9 98.2 %reduce-scatter.8.cloned.1.call-start = ((), (), s32[]{:S(2)}) async-start(), calls=%async_computation.4 | async-start | bytes 2359296 | tf_op jit(solution)/shard_map/reduce_scatter | solution.py:32
  70.0 69.7 %reduce-scatter.10.cloned.1.call-start = ((), (), s32[]{:S(2)}) async-start(), calls=%async_computation.6 | async-start | bytes 1179648
  74.5 94.1 %all-gather.6.cloned.1.call-start = ((), (), s32[]{:S(2)}) async-start(), calls=%async_computation.5 | async-start | bytes 2359296 | tf_op jit(solution)/shard_map/all_gather | solution.py:42
  106.1 124.2 %copy-start.1 = (f32[256,256]{1,0:T(8,128)S(1)}, f32[256,256]{1,0:T(8,128)}, u32[]{:S(2)}) copy-start(f32[256,256]{1,0:T(8,128)} %reduce-scatter.8.cloned.1.call-done) | copy-start | bytes 786436
  108.6 300.0 %reduce-scatter.12.cloned.1.call-start = ((), (), s32[]{:S(2)}) async-start(), calls=%async_computation.7 | async-start | bytes 655360
  271.2 4.7 %collective-permute-start = (f32[4,256]{1,0:T(4,128)S(1)}, f32[4,256]{1,0:T(4,128)S(1)}, u32[]{:S(2)}, u32[]{:S(2)}) collective-permute-start(f32[4,256]{1,0:T(4,128)S(1)} %fusion.104), channel_id=1, source_target_pairs={{0,8},{8,16},{16,24},{1,9},{9,17},{17,25},{2,10},{10,18},{18,26},{... | collective-permute-start | bytes 12296 | tf_op jit(solution)/shard_map/while/body/eval_jaxpr/ppermute | solution.py:10
  315.0 5.6 %collective-permute-start = (f32[4,256]{1,0:T(4,128)S(1)}, f32[4,256]{1,0:T(4,128)S(1)}, u32[]{:S(2)}, u32[]{:S(2)}) collective-permute-start(f32[4,256]{1,0:T(4,128)S(1)} %fusion.104), channel_id=1, source_target_pairs={{0,8},{8,16},{16,24},{1,9},{9,17},{17,25},{2,10},{10,18},{18,26},{... | collective-permute-start | bytes 12296 | tf_op jit(solution)/shard_map/while/body/eval_jaxpr/ppermute | solution.py:10
  359.7 5.6 %collective-permute-start = (f32[4,256]{1,0:T(4,128)S(1)}, f32[4,256]{1,0:T(4,128)S(1)}, u32[]{:S(2)}, u32[]{:S(2)}) collective-permute-start(f32[4,256]{1,0:T(4,128)S(1)} %fusion.104), channel_id=1, source_target_pairs={{0,8},{8,16},{16,24},{1,9},{9,17},{17,25},{2,10},{10,18},{18,26},{... | collective-permute-start | bytes 12296 | tf_op jit(solution)/shard_map/while/body/eval_jaxpr/ppermute | solution.py:10
  380.3 30.0 %copy-start.2 = (f32[4,256]{1,0:T(4,128)}, f32[4,256]{1,0:T(4,128)S(1)}, u32[]{:S(2)}) copy-start(f32[4,256]{1,0:T(4,128)S(1)} %bitcast_select_fusion.1) | copy-start | bytes 12292
Sparse Core Ops, SparseCore 0:
  9.8 55.2 all-gather.3
  70.1 35.9 reduce-scatter.7
  108.4 31.2 reduce-scatter.9
  141.2 27.3 all-gather.5
  381.6 25.7 reduce-scatter.11
